TPU v7x, 32 devices: a whole 2x2x4 slice. The times are simulated.
32 devices in a mesh: section: 4 (over y, x), seq: 8 (over z, core).
Axes of the slice: x: 2, y: 2, z: 4, core: 2. Of those that a mesh axis runs over, the one named last changes fastest.
Arguments:
- queries: bfloat16 [4, 1024, 4096], P('section', 'seq'), may hold values from -500 to 500
- keys: bfloat16 [4, 1024, 512], P('section', 'seq'), may hold values from -6 to 6
- values: bfloat16 [4, 1024, 512], P('section', 'seq'), may hold values from -6 to 6
- out_grad: bfloat16 [4, 1024, 4096], P('section', 'seq'), may hold values from -6 to 6
- documents: int32 [4, 1024], P('section'), may hold values from 0 to 3, never falling along the last dimension, each value on 1 to 512 neighbouring positions
- query_weight: bfloat16 [4, 4096, 4096], P('section', 'seq'), may hold values from -0.09375 to 0.09375
- key_weight: bfloat16 [4, 512, 4096], P('section'), may hold values from -0.1875 to 0.1875
- value_weight: bfloat16 [4, 512, 4096], P('section'), may hold values from -0.1875 to 0.1875
Outputs:
- upstream: bfloat16 [4, 1024, 4096], P('section', 'seq')
Inputs may be any that keep to these rules, and one draw needn't show every extreme that they name: `documents`: each section's document ids never fall along its tokens.
All inputs are finite; a program needn't handle non-finite values.
Results may differ from a plain program's by a relative error of at most 0.0058.
Values may be sent and summed in bfloat16 or wider, within the bound.
No kernel may reach another device: no remote copies, remote signals or barrier semaphores. Data moves between devices by JAX's collectives and lax.ppermute only.
A program may use at most 192 MiB of HBM per device.

v0:
```python
import math

import jax
import jax.numpy as jnp
from jax import lax
from jax.sharding import PartitionSpec as P

KV = 4
HD = 128


def passed_along(block, axis, distance):
    devices = range(lax.axis_size(axis))
    route = [(i - distance, i) for i in devices if i - distance in devices]
    return lax.ppermute(block, axis, route)


def body(queries, keys, values, out_grad, documents, query_weight, key_weight, value_weight):
    count = lax.axis_size("seq")
    tok = queries.shape[1]
    total = tok * count
    heads_here = query_weight.shape[1] // HD
    reps = count // KV
    scale = 1.0 / math.sqrt(HD)
    q_send = queries[0].reshape(tok, count, heads_here * HD)
    o_send = out_grad[0].reshape(tok, count, heads_here * HD)
    q_all, o_all = (
        lax.all_to_all(q_send, "seq", split_axis=1, concat_axis=0, tiled=True),
        lax.all_to_all(o_send, "seq", split_axis=1, concat_axis=0, tiled=True),
    )
    q_all = q_all.reshape(total, heads_here, HD)
    o_all = o_all.reshape(total, heads_here, HD)
    k_rep = jnp.repeat(keys[0].reshape(tok, KV, HD), reps, axis=1)
    v_rep = jnp.repeat(values[0].reshape(tok, KV, HD), reps, axis=1)
    k_head, v_head = (
        lax.all_to_all(k_rep, "seq", split_axis=1, concat_axis=0, tiled=True),
        lax.all_to_all(v_rep, "seq", split_axis=1, concat_axis=0, tiled=True),
    )
    k_head = k_head.reshape(total, HD)
    v_head = v_head.reshape(total, HD)
    doc_ids = documents[0]
    block = min(512, total)
    columns = lax.iota(jnp.int32, total)

    def attend(carry, index):
        dkey, dvalue = carry
        first = index * block
        q_blk = lax.dynamic_slice_in_dim(q_all, first, block, 0)
        o_blk = lax.dynamic_slice_in_dim(o_all, first, block, 0)
        rows = first + lax.iota(jnp.int32, block)
        row_ids = lax.dynamic_slice_in_dim(doc_ids, first, block, 0)
        allowed = (columns[None, :] <= rows[:, None]) & (doc_ids[None, :] == row_ids[:, None])
        scores = (
            jnp.einsum("bhd,td->hbt", q_blk, k_head, preferred_element_type=jnp.float32) * scale
        )
        scores = jnp.where(allowed[None], scores, -jnp.inf)
        top = jnp.max(scores, axis=-1, keepdims=True)
        expo = jnp.exp(scores - top)
        prob = expo / jnp.sum(expo, axis=-1, keepdims=True)
        prob_low = prob.astype(jnp.bfloat16)
        dprob = jnp.einsum("bhd,td->hbt", o_blk, v_head, preferred_element_type=jnp.float32)
        delta = jnp.sum(prob * dprob, axis=-1, keepdims=True)
        dscore = (prob * (dprob - delta) * scale).astype(jnp.bfloat16)
        dq_blk = jnp.einsum(
            "hbt,td->bhd", dscore, k_head, preferred_element_type=jnp.float32
        ).astype(jnp.bfloat16)
        dkey = dkey + jnp.einsum("hbt,bhd->td", dscore, q_blk, preferred_element_type=jnp.float32)
        dvalue = dvalue + jnp.einsum(
            "hbt,bhd->td", prob_low, o_blk, preferred_element_type=jnp.float32
        )
        return ((dkey, dvalue), dq_blk)

    start_carry = (jnp.zeros((total, HD), jnp.float32), jnp.zeros((total, HD), jnp.float32))
    (dkey, dvalue), dq_blocks = lax.scan(
        attend, start_carry, jnp.arange(total // block, dtype=jnp.int32)
    )
    dquery = dq_blocks.reshape(total, heads_here * HD)
    dkey_low = dkey.astype(jnp.bfloat16)
    dvalue_low = dvalue.astype(jnp.bfloat16)
    dq_tok, dk_tok, dv_tok = (
        lax.all_to_all(
            dquery.reshape(total, 1, heads_here * HD),
            "seq",
            split_axis=0,
            concat_axis=1,
            tiled=True,
        ),
        lax.all_to_all(
            dkey_low.reshape(total, 1, HD), "seq", split_axis=0, concat_axis=1, tiled=True
        ),
        lax.all_to_all(
            dvalue_low.reshape(total, 1, HD), "seq", split_axis=0, concat_axis=1, tiled=True
        ),
    )
    dq_tok = dq_tok.reshape(tok, count * heads_here * HD)
    dk_tok = dk_tok.reshape(tok, count * HD)
    dv_tok = dv_tok.reshape(tok, count * HD)
    wk_rep = jnp.repeat(key_weight[0].reshape(KV, HD, -1), reps, axis=0).reshape(count * HD, -1)
    wv_rep = jnp.repeat(value_weight[0].reshape(KV, HD, -1), reps, axis=0).reshape(count * HD, -1)
    start_sum = jnp.dot(dk_tok, wk_rep, preferred_element_type=jnp.float32)
    start_sum = start_sum + jnp.dot(dv_tok, wv_rep, preferred_element_type=jnp.float32)
    dinput = start_sum + jnp.dot(
        dq_tok,
        lax.all_gather(query_weight[0], "seq", axis=0, tiled=True),
        preferred_element_type=jnp.float32,
    )
    dinput = dinput.astype(jnp.bfloat16)
    received = passed_along(dinput, "section", -1)
    return received[None]


def solution(mesh):
    in_specs = (
        P("section", "seq", None),
        P("section", "seq", None),
        P("section", "seq", None),
        P("section", "seq", None),
        P("section", None),
        P("section", "seq", None),
        P("section", None, None),
        P("section", None, None),
    )
    out_specs = P("section", "seq", None)
    return jax.shard_map(body, mesh=mesh, in_specs=in_specs, out_specs=out_specs, check_vma=False)
```

profile of v0, /device:TPU:0, one launch (start us, length us, event | category | flops | bytes accessed | tf_op | source)
XLA Modules:
  0.0 433.7 jit_solution(672726303252246511)
XLA Ops:
  6.5 0.7 all-gather.3.cloned.1.call-update
  7.3 0.9 reshape_squeeze.21
  8.2 0.7 broadcast_in_dim.43
  9.0 6.4 %all-to-all-start.3 = ((bf16[128,8,128]{2,0,1:T(8,128)(2,1)}), bf16[128,8,128]{2,0,1:T(8,128)(2,1)S(1)}, u32[]{:S(2)}, u32[]{:S(2)}) async-start(bf16[128,8,128]{2,0,1:T(8,128)(2,1)} %bitcast.11), calls=%async_computation.3 | async-start | bytes 524288 | tf_op jit(solution)/shard_map/all_to_all | solution.py:37
  15.3 2.3 copy.52
  17.6 7.4 %all-to-all-done.3 = bf16[128,8,128]{2,0,1:T(8,128)(2,1)S(1)} async-done(((bf16[128,8,128]{2,0,1:T(8,128)(2,1)}), bf16[128,8,128]{2,0,1:T(8,128)(2,1)S(1)}, u32[]{:S(2)}, u32[]{:S(2)}) %all-to-all-start.3) | async-done | bytes 262176 | tf_op jit(solution)/shard_map/all_to_all | solution.py:37
  25.0 3.6 all-to-all-start
  28.7 1.3 copy.55
  30.0 54.5 %all-to-all-done = bf16[128,8,512]{0,2,1:T(8,128)(2,1)S(1)} async-done(((bf16[128,8,512]{0,2,1:T(8,128)(2,1)}), bf16[128,8,512]{0,2,1:T(8,128)(2,1)S(1)}, u32[]{:S(2)}, u32[]{:S(2)}) %all-to-all-start) | async-done | bytes 1048608 | tf_op jit(solution)/shard_map/all_to_all | solution.py:28
  84.5 3.6 all-to-all-start.2
  88.1 58.2 %all-to-all-done.2 = bf16[128,8,512]{0,2,1:T(8,128)(2,1)S(1)} async-done(((bf16[128,8,512]{0,2,1:T(8,128)(2,1)}), bf16[128,8,512]{0,2,1:T(8,128)(2,1)S(1)}, u32[]{:S(2)}, u32[]{:S(2)}) %all-to-all-start.2) | async-done | bytes 1048608 | tf_op jit(solution)/shard_map/all_to_all | solution.py:29
  146.3 0.7 broadcast_in_dim.42
  147.0 3.4 all-to-all-start.1
  150.5 1.7 copy.53
  152.2 2.4 reshape.106
  154.5 1.7 copy.56
  156.2 1.5 reshape.109
  157.7 13.9 %all-to-all-done.1 = bf16[128,8,128]{2,0,1:T(8,128)(2,1)S(1)} async-done(((bf16[128,8,128]{2,0,1:T(8,128)(2,1)}), bf16[128,8,128]{2,0,1:T(8,128)(2,1)S(1)}, u32[]{:S(2)}, u32[]{:S(2)}) %all-to-all-start.1) | async-done | bytes 262176 | tf_op jit(solution)/shard_map/all_to_all | solution.py:36
  171.6 114.2 %while.15 = (s32[]{:T(128)}, f32[1024,128]{1,0:T(8,128)}, f32[1024,128]{1,0:T(8,128)}, bf16[2,512,4,128]{3,2,1,0:T(4,128)(2,1)}, s32[2]{0:T(128)S(1)}, /*index=5...) while((s32[]{:T(128)}, f32[1024,128]{1,0:T(8,128)}, ...), condition=%wide.region_4.5_spmd.clone, body=%wide.region_0.4_spmd.clone.sunk | while | flops 2728664576 | bytes 95738200 | solution.py:74
  171.6 0.6 dynamic_slice.45
  172.8 0.5 fusion.108
  173.3 7.4 %fusion.109 = (f32[4,512]{1,0:T(4,128)S(1)}, f32[4,512,1024]{2,1,0:T(8,128)}) fusion(pred[512,1024]{1,0:T(8,128)(4,1)S(1)} %fusion.108, bf16[1024,4,128]{0,2,1:T(8,128)(2,1)} %get-tuple-element.288, s32[]{:T(128)S(6)} %select_n.30, bf16[1024,128]{1,0:T(8,128)(2,1)S(1)} %get-tuple-element.289), kind=kOutput, calls=%fused_computation.62.clone.1 | convolution fusion | flops 545260544 | bytes 9707524 | tf_op jit(solution)/shard_map/while/body/eval_jaxpr/sub | solution.py:58
  180.7 4.5 %fusion.107 = f32[512,4,1024]{2,0,1:T(8,128)} fusion(bf16[1024,4,128]{0,2,1:T(8,128)(2,1)S(1)} %get-tuple-element.290, s32[]{:T(128)S(6)} %select_n.30, bf16[1024,128]{1,0:T(8,128)(2,1)S(1)} %get-tuple-element.291), kind=kOutput, calls=%fused_computation.32.clone.1 | convolution fusion | flops 536870912 | bytes 9175044 | tf_op jit(solution)/shard_map/while/body/eval_jaxpr/bhd,td->hbt/dot_general | solution.py:61
  185.2 16.6 %fusion.112 = bf16[1,512,4,128]{3,1,2,0:T(8,128)(2,1)S(1)} fusion(f32[512,4,1024]{2,0,1:T(8,128)} %fusion.107, bf16[1024,128]{1,0:T(8,128)(2,1)S(1)} %get-tuple-element.289, f32[4,512,1024]{2,1,0:T(8,128)} %get-tuple-element.249, f32[4,512]{1,0:T(4,128)S(1)} %get-tuple-element.250), kind=kOutput, calls=%fused_computation.25.clone.1 | convolution fusion | flops 551816192 | bytes 17571840 | tf_op jit(solution)/shard_map/while/body/eval_jaxpr/hbt,td->bhd/dot_general | solution.py:64
  201.8 0.4 copy_dynamic-update-slice_fusion.2
  202.3 6.3 %fusion.111 = f32[1024,128]{1,0:T(8,128)} fusion(f32[1024,128]{1,0:T(8,128)} %get-tuple-element.268, bf16[1024,4,128]{0,2,1:T(8,128)(2,1)S(1)} %get-tuple-element.290, s32[]{:T(128)S(6)} %select_n.30, pred[]{:T(512)S(6)} %compare.3, f32[4,512,1024]{2,1,0:T(8,128)} %get-tuple-element.249, f32[4,512]{1,0:T(4,128)S(1)} %get-tuple-element.250), kind=kOutput, calls=%fused_computation.28.clone.1 | convolution fusion | flops 541327360 | bytes 9969669 | tf_op jit(solution)/shard_map/while/body/eval_jaxpr/hbt,bhd->td/dot_general | solution.py:68
  208.6 19.1 %fusion.110 = f32[1024,128]{1,0:T(8,128)S(1)} fusion(f32[512,4,1024]{2,0,1:T(8,128)} %fusion.107, f32[1024,128]{1,0:T(8,128)S(1)} %copy-done.5, bf16[1024,4,128]{0,2,1:T(8,128)(2,1)} %get-tuple-element.288, s32[]{:T(128)S(6)} %select_n.30, pred[]{:T(512)S(6)} %compare.3, f32[4,512,1024]{2,1,0:T(8,128)} %get-tuple-element.249, ...), kind=kOutput, calls=%fused_computation.29.clone.1 | convolution fusion | flops 551816192 | bytes 35143684 | tf_op jit(solution)/shard_map/while/body/eval_jaxpr/hbt,bhd->td/dot_general | solution.py:67
  227.7 0.8 copy-done.6
  228.5 0.6 dynamic_slice.45
  229.7 0.5 fusion.108
  230.2 7.4 %fusion.109 = (f32[4,512]{1,0:T(4,128)S(1)}, f32[4,512,1024]{2,1,0:T(8,128)}) fusion(pred[512,1024]{1,0:T(8,128)(4,1)S(1)} %fusion.108, bf16[1024,4,128]{0,2,1:T(8,128)(2,1)} %get-tuple-element.288, s32[]{:T(128)S(6)} %select_n.30, bf16[1024,128]{1,0:T(8,128)(2,1)S(1)} %get-tuple-element.289), kind=kOutput, calls=%fused_computation.62.clone.1 | convolution fusion | flops 545260544 | bytes 9707524 | tf_op jit(solution)/shard_map/while/body/eval_jaxpr/sub | solution.py:58
  237.6 4.5 %fusion.107 = f32[512,4,1024]{2,0,1:T(8,128)} fusion(bf16[1024,4,128]{0,2,1:T(8,128)(2,1)S(1)} %get-tuple-element.290, s32[]{:T(128)S(6)} %select_n.30, bf16[1024,128]{1,0:T(8,128)(2,1)S(1)} %get-tuple-element.291), kind=kOutput, calls=%fused_computation.32.clone.1 | convolution fusion | flops 536870912 | bytes 9175044 | tf_op jit(solution)/shard_map/while/body/eval_jaxpr/bhd,td->hbt/dot_general | solution.py:61
  242.1 16.6 %fusion.112 = bf16[1,512,4,128]{3,1,2,0:T(8,128)(2,1)S(1)} fusion(f32[512,4,1024]{2,0,1:T(8,128)} %fusion.107, bf16[1024,128]{1,0:T(8,128)(2,1)S(1)} %get-tuple-element.289, f32[4,512,1024]{2,1,0:T(8,128)} %get-tuple-element.249, f32[4,512]{1,0:T(4,128)S(1)} %get-tuple-element.250), kind=kOutput, calls=%fused_computation.25.clone.1 | convolution fusion | flops 551816192 | bytes 17571840 | tf_op jit(solution)/shard_map/while/body/eval_jaxpr/hbt,td->bhd/dot_general | solution.py:64
  258.7 0.4 copy_dynamic-update-slice_fusion.2
  259.2 6.5 %fusion.111 = f32[1024,128]{1,0:T(8,128)} fusion(f32[1024,128]{1,0:T(8,128)} %get-tuple-element.268, bf16[1024,4,128]{0,2,1:T(8,128)(2,1)S(1)} %get-tuple-element.290, s32[]{:T(128)S(6)} %select_n.30, pred[]{:T(512)S(6)} %compare.3, f32[4,512,1024]{2,1,0:T(8,128)} %get-tuple-element.249, f32[4,512]{1,0:T(4,128)S(1)} %get-tuple-element.250), kind=kOutput, calls=%fused_computation.28.clone.1 | convolution fusion | flops 541327360 | bytes 9969669 | tf_op jit(solution)/shard_map/while/body/eval_jaxpr/hbt,bhd->td/dot_general | solution.py:68
  265.8 19.1 %fusion.110 = f32[1024,128]{1,0:T(8,128)S(1)} fusion(f32[512,4,1024]{2,0,1:T(8,128)} %fusion.107, f32[1024,128]{1,0:T(8,128)S(1)} %copy-done.5, bf16[1024,4,128]{0,2,1:T(8,128)(2,1)} %get-tuple-element.288, s32[]{:T(128)S(6)} %select_n.30, pred[]{:T(512)S(6)} %compare.3, f32[4,512,1024]{2,1,0:T(8,128)} %get-tuple-element.249, ...), kind=kOutput, calls=%fused_computation.29.clone.1 | convolution fusion | flops 551816192 | bytes 35143684 | tf_op jit(solution)/shard_map/while/body/eval_jaxpr/hbt,bhd->td/dot_general | solution.py:67
  284.9 0.8 copy-done.6
  285.7 1.3 convert_bitcast_fusion
  287.0 0.5 broadcast.93
  287.5 0.7 reduce
  288.2 0.8 reshape.122
  289.0 3.4 all-to-all-start.4
  292.4 0.7 reduce.1
  293.1 0.8 reshape.124
  293.9 17.0 %all-to-all-done.4 = bf16[8,2,8192]{2,1,0:T(2,128)(2,1)S(1)} async-done(((bf16[8,2,8192]{2,1,0:T(2,128)(2,1)}), bf16[8,2,8192]{2,1,0:T(2,128)(2,1)S(1)}, u32[]{:S(2)}, u32[]{:S(2)}) %all-to-all-start.4) | async-done | bytes 262176 | tf_op jit(solution)/shard_map/all_to_all | solution.py:88
  310.9 4.0 all-to-all-start.5
  314.9 5.9 %reshape_reshape.12 = bf16[1024,1,512]{2,1,0:T(2,128)(2,1)S(1)} reshape(bf16[2,512,4,128]{3,2,1,0:T(4,128)(2,1)} %get-tuple-element.71) | data formatting | bytes 2097152 | tf_op jit(solution)/shard_map/reshape;reshape | solution.py:82
  320.8 6.9 %reduce.2 = bf16[1024,512]{1,0:T(8,128)(2,1)S(1)} reduce(bf16[1024,1,512]{2,1,0:T(2,128)(2,1)S(1)} %reshape_reshape.12, bf16[]{:T(256)} %broadcast.93), dimensions={1}, to_apply=%reshape_reshape.12.reduce_sub_computation | reduce | bytes 2097154 | tf_op jit(solution)/shard_map/reshape;reshape | solution.py:82
  327.7 1.6 reshape.126
  329.3 8.4 %all-to-all-done.5 = bf16[8,2,8192]{2,1,0:T(2,128)(2,1)} async-done(((bf16[8,2,8192]{2,1,0:T(2,128)(2,1)}), bf16[8,2,8192]{2,1,0:T(2,128)(2,1)}, u32[]{:S(2)}, u32[]{:S(2)}) %all-to-all-start.5) | async-done | bytes 262176 | tf_op jit(solution)/shard_map/all_to_all | solution.py:91
  337.7 4.5 %all-to-all-start.6 = ((bf16[8,2,32768]{2,1,0:T(2,128)(2,1)}), bf16[8,2,32768]{2,1,0:T(2,128)(2,1)}, u32[]{:S(2)}, u32[]{:S(2)}) async-start(bf16[8,2,32768]{2,1,0:T(2,128)(2,1)} %reshape.126), calls=%async_computation.6 | async-start | bytes 2097152 | tf_op jit(solution)/shard_map/all_to_all | solution.py:81
  342.7 1.2 reshape.125
  344.0 0.9 copy.63
  344.8 6.5 %broadcast_in_dim.44 = bf16[4,2,128,4096]{3,2,1,0:T(8,128)(2,1)} broadcast(bf16[4,128,4096]{2,1,0:T(8,128)(2,1)} %bitcast.171), dimensions={0,2,3} | broadcast | bytes 12582912 | tf_op jit(solution)/shard_map/broadcast_in_dim | solution.py:98
  351.3 4.8 %fusion.79 = f32[128,4096]{1,0:T(8,128)S(1)} fusion(bf16[128,1024]{0,1:T(8,128)(2,1)S(1)} %bitcast.177, bf16[1024,4096]{1,0:T(8,128)(2,1)} %bitcast.168), kind=kOutput, calls=%fused_computation.63 | convolution fusion | flops 1073741824 | bytes 10747904 | tf_op jit(solution)/shard_map/dot_general | solution.py:100
  356.2 4.3 broadcast_in_dim.45
  360.4 6.1 %convolution_add_fusion = f32[128,4096]{1,0:T(8,128)} fusion(f32[128,4096]{1,0:T(8,128)S(1)} %fusion.79, bf16[128,1024]{0,1:T(8,128)(2,1)S(1)} %bitcast.178, bf16[1024,4096]{1,0:T(8,128)(2,1)} %bitcast.167), kind=kOutput, calls=%fused_computation.58 | convolution fusion | flops 1074266112 | bytes 12845056 | tf_op jit(solution)/shard_map/dot_general | solution.py:101
  366.5 13.7 %all-to-all-done.6 = bf16[8,2,32768]{2,1,0:T(2,128)(2,1)} async-done(((bf16[8,2,32768]{2,1,0:T(2,128)(2,1)}), bf16[8,2,32768]{2,1,0:T(2,128)(2,1)}, u32[]{:S(2)}, u32[]{:S(2)}) %all-to-all-start.6) | async-done | bytes 1048608 | tf_op jit(solution)/shard_map/all_to_all | solution.py:81
  380.2 4.3 reshape.127
  384.8 0.7 copy.66
  385.5 13.8 %fusion.67 = bf16[128,4096]{1,0:T(8,128)(2,1)S(1)} fusion(f32[128,4096]{1,0:T(8,128)} %convolution_add_fusion, bf16[128,4096]{0,1:T(8,128)(2,1)S(1)} %bitcast.170, bf16[1,4096,4096]{2,1,0:T(8,128)(2,1)} %all-gather.3.cloned.1.call-done), kind=kOutput, calls=%fused_computation.59 | convolution fusion | flops 4296015872 | bytes 37748736 | tf_op jit(solution)/shard_map/dot_general | solution.py:102
  399.3 1.3 collective-permute-start
  400.6 25.3 %collective-permute-done = bf16[128,4096]{1,0:T(8,128)(2,1)S(1)} collective-permute-done((bf16[128,4096]{1,0:T(8,128)(2,1)S(1)}, bf16[128,4096]{1,0:T(8,128)(2,1)S(1)}, u32[]{:S(2)}, u32[]{:S(2)}) %collective-permute-start) | collective-permute-done | bytes 1048608 | tf_op jit(solution)/shard_map/ppermute | solution.py:15
  425.9 1.0 copy.95
  (42 shorter events, 1.1 us)
Async XLA Ops:
  6.5 22.1 %copy-start.4 = (bf16[1,128,4096]{2,1,0:T(8,128)(2,1)S(1)}, bf16[1,128,4096]{2,1,0:T(8,128)(2,1)}, u32[]{:S(2)}) copy-start(bf16[1,128,4096]{2,1,0:T(8,128)(2,1)} %param.13) | copy-start | bytes 3145732
  6.5 81.5 %copy-start.8 = (bf16[1,128,512]{2,1,0:T(8,128)(2,1)S(1)}, bf16[1,128,512]{2,1,0:T(8,128)(2,1)}, u32[]{:S(2)}) copy-start(bf16[1,128,512]{2,1,0:T(8,128)(2,1)} %param.11) | copy-start | bytes 393220
  6.5 378.9 %all-gather.3.cloned.1.call-start = ((), (), s32[]{:S(2)}) async-start(), calls=%async_computation.7 | async-start | bytes 37748736 | tf_op jit(solution)/shard_map/all_gather | solution.py:104
  9.0 16.1 %all-to-all-start.3 = ((bf16[128,8,128]{2,0,1:T(8,128)(2,1)}), bf16[128,8,128]{2,0,1:T(8,128)(2,1)S(1)}, u32[]{:S(2)}, u32[]{:S(2)}) async-start(bf16[128,8,128]{2,0,1:T(8,128)(2,1)} %bitcast.11), calls=%async_computation.3 | async-start | bytes 524288 | tf_op jit(solution)/shard_map/all_to_all | solution.py:37
  17.6 154.0 %copy-start.7 = (s32[1,1024]{1,0:T(1,128)S(1)}, s32[1,1024]{1,0:T(1,128)}, u32[]{:S(2)}) copy-start(s32[1,1024]{1,0:T(1,128)} %param.14) | copy-start | bytes 12292
  25.0 59.4 %all-to-all-start = ((bf16[128,8,512]{0,2,1:T(8,128)(2,1)}), bf16[128,8,512]{0,2,1:T(8,128)(2,1)S(1)}, u32[]{:S(2)}, u32[]{:S(2)}) async-start(bf16[128,8,512]{0,2,1:T(8,128)(2,1)} %bitcast.1), calls=%async_computation | async-start | bytes 2097152 | tf_op jit(solution)/shard_map/all_to_all | solution.py:28
  84.5 61.8 %all-to-all-start.2 = ((bf16[128,8,512]{0,2,1:T(8,128)(2,1)}), bf16[128,8,512]{0,2,1:T(8,128)(2,1)S(1)}, u32[]{:S(2)}, u32[]{:S(2)}) async-start(bf16[128,8,512]{0,2,1:T(8,128)(2,1)} %bitcast.176), calls=%async_computation.2 | async-start | bytes 2097152 | tf_op jit(solution)/shard_map/all_to_all | solution.py:29
  147.0 24.5 %all-to-all-start.1 = ((bf16[128,8,128]{2,0,1:T(8,128)(2,1)}), bf16[128,8,128]{2,0,1:T(8,128)(2,1)S(1)}, u32[]{:S(2)}, u32[]{:S(2)}) async-start(bf16[128,8,128]{2,0,1:T(8,128)(2,1)} %bitcast.4), calls=%async_computation.1 | async-start | bytes 524288 | tf_op jit(solution)/shard_map/all_to_all | solution.py:36
  185.2 16.7 %copy-start.2 = (bf16[2,512,4,128]{3,2,1,0:T(4,128)(2,1)S(1)}, bf16[2,512,4,128]{3,2,1,0:T(4,128)(2,1)}, u32[]{:S(2)}) copy-start(bf16[2,512,4,128]{3,2,1,0:T(4,128)(2,1)} %get-tuple-element.269) | copy-start | bytes 3145732 | tf_op jit(solution)/shard_map/while
  202.3 6.3 %copy-start.3 = (bf16[2,512,4,128]{3,2,1,0:T(4,128)(2,1)}, bf16[2,512,4,128]{3,2,1,0:T(4,128)(2,1)S(1)}, u32[]{:S(2)}) copy-start(bf16[2,512,4,128]{3,2,1,0:T(4,128)(2,1)S(1)} %copy_dynamic-update-slice_fusion.2) | copy-start | bytes 3145732 | tf_op jit(solution)/shard_map/while
  202.3 6.3 %copy-start.5 = (f32[1024,128]{1,0:T(8,128)S(1)}, f32[1024,128]{1,0:T(8,128)}, u32[]{:S(2)}) copy-start(f32[1024,128]{1,0:T(8,128)} %get-tuple-element.267) | copy-start | bytes 1572868 | tf_op jit(solution)/shard_map/while
  227.7 0.8 copy-start.6
  242.1 16.6 %copy-start.2 = (bf16[2,512,4,128]{3,2,1,0:T(4,128)(2,1)S(1)}, bf16[2,512,4,128]{3,2,1,0:T(4,128)(2,1)}, u32[]{:S(2)}) copy-start(bf16[2,512,4,128]{3,2,1,0:T(4,128)(2,1)} %get-tuple-element.269) | copy-start | bytes 3145732 | tf_op jit(solution)/shard_map/while
  259.2 6.6 %copy-start.3 = (bf16[2,512,4,128]{3,2,1,0:T(4,128)(2,1)}, bf16[2,512,4,128]{3,2,1,0:T(4,128)(2,1)S(1)}, u32[]{:S(2)}) copy-start(bf16[2,512,4,128]{3,2,1,0:T(4,128)(2,1)S(1)} %copy_dynamic-update-slice_fusion.2) | copy-start | bytes 3145732 | tf_op jit(solution)/shard_map/while
  259.2 6.6 %copy-start.5 = (f32[1024,128]{1,0:T(8,128)S(1)}, f32[1024,128]{1,0:T(8,128)}, u32[]{:S(2)}) copy-start(f32[1024,128]{1,0:T(8,128)} %get-tuple-element.267) | copy-start | bytes 1572868 | tf_op jit(solution)/shard_map/while
  284.9 0.8 copy-start.6
  289.0 21.9 %all-to-all-start.4 = ((bf16[8,2,8192]{2,1,0:T(2,128)(2,1)}), bf16[8,2,8192]{2,1,0:T(2,128)(2,1)S(1)}, u32[]{:S(2)}, u32[]{:S(2)}) async-start(bf16[8,2,8192]{2,1,0:T(2,128)(2,1)} %reshape.122), calls=%async_computation.4 | async-start | bytes 524288 | tf_op jit(solution)/shard_map/all_to_all | solution.py:88
  310.9 26.8 %all-to-all-start.5 = ((bf16[8,2,8192]{2,1,0:T(2,128)(2,1)}), bf16[8,2,8192]{2,1,0:T(2,128)(2,1)}, u32[]{:S(2)}, u32[]{:S(2)}) async-start(bf16[8,2,8192]{2,1,0:T(2,128)(2,1)} %reshape.124), calls=%async_computation.5 | async-start | bytes 524288 | tf_op jit(solution)/shard_map/all_to_all | solution.py:91
  337.7 42.5 %all-to-all-start.6 = ((bf16[8,2,32768]{2,1,0:T(2,128)(2,1)}), bf16[8,2,32768]{2,1,0:T(2,128)(2,1)}, u32[]{:S(2)}, u32[]{:S(2)}) async-start(bf16[8,2,32768]{2,1,0:T(2,128)(2,1)} %reshape.126), calls=%async_computation.6 | async-start | bytes 2097152 | tf_op jit(solution)/shard_map/all_to_all | solution.py:81
  351.3 4.8 %copy-start = (bf16[1,512,4096]{2,1,0:T(8,128)(2,1)S(1)}, bf16[1,512,4096]{2,1,0:T(8,128)(2,1)}, u32[]{:S(2)}) copy-start(bf16[1,512,4096]{2,1,0:T(8,128)(2,1)} %param.17) | copy-start | bytes 12582916
  356.1 4.3 copy-start.1
  399.3 26.6 %collective-permute-start = (bf16[128,4096]{1,0:T(8,128)(2,1)S(1)}, bf16[128,4096]{1,0:T(8,128)(2,1)S(1)}, u32[]{:S(2)}, u32[]{:S(2)}) collective-permute-start(bf16[128,4096]{1,0:T(8,128)(2,1)S(1)} %fusion.67), channel_id=1, source_target_pairs={{8,0},{16,8},{24,16},{9,1},{17,9},{25,17},{10,2},{18,10},{26,18},{... | collective-permute-start | bytes 3145736 | tf_op jit(solution)/shard_map/ppermute | solution.py:15
Sparse Core Ops, SparseCore 0:
  8.9 375.4 all-gather.2
where the time goes:
time: 435 us; the launch traced here: 434 us
  waiting for transfers between devices  199 us (46%)
  matrix products  133 us (31%)
  local copies, waits for them, and re-layouts  46.1 us (11%)
  starting transfers between devices  30.2 us (7%)
  between operations  13.7 us (3%)
  other arithmetic  10.6 us (2%)
    all_to_all x1, waiting for transfers between devices, body(): lax.all_to_all(o_send, 'seq', split_axis=1, concat_axis=0, tiled=True)  58.2 us
    all_to_all x1, waiting for transfers between devices, body(): lax.all_to_all(q_send, 'seq', split_axis=1, concat_axis=0, tiled=True)  54.5 us
    dot_general x2, matrix products, attend(): jnp.einsum('hbt,bhd->td', dscore, q_blk, preferred_element_type=jnp.float32)  38.3 us
    dot_general x2, matrix products, attend(): jnp.einsum('hbt,td->bhd', dscore, k_head, preferred_element_type=jnp.floa...  33.3 us
    ppermute x1, waiting for transfers between devices, passed_along(): return lax.ppermute(block, axis, route)  25.3 us
    all_to_all x1, waiting for transfers between devices, body(): lax.all_to_all(dkey_low.reshape(total, 1, HD), 'seq', split_axis=0, conca...  17 us
    sub x2, matrix products, attend(): expo = jnp.exp(scores - top)  14.8 us
    all_to_all x1, waiting for transfers between devices, body(): lax.all_to_all(k_rep, 'seq', split_axis=1, concat_axis=0, tiled=True)  13.9 us
  transfers between devices with their start and end apart: 9, of which 8 were waited for; matrix products, arithmetic and copies ran while one was open for 40% of the time, Pallas kernels for 0%

commit v1 on v0

v1 whole, which is shorter than its diff:
```python
import functools
import math

import jax
import jax.numpy as jnp
from jax import lax
from jax.experimental import pallas as pl
from jax.experimental.pallas import tpu as pltpu
from jax.sharding import PartitionSpec as P

HD = 128
CHUNKS = 2


def passed_along(block, axis, distance):
    devices = range(lax.axis_size(axis))
    route = [(i - distance, i) for i in devices if i - distance in devices]
    return lax.ppermute(block, axis, route)


def attend_kernel(start_ref, q_ref, o_ref, k_ref, v_ref, out_ref, dk_acc, dv_acc, *, heads, block):
    head = pl.program_id(0)
    total = k_ref.shape[0]
    scale = 1.0 / math.sqrt(HD)
    nt = (((1,), (1,)), ((), ()))
    tn = (((0,), (0,)), ((), ()))

    @pl.when(head == 0)
    def _():
        dk_acc[...] = jnp.zeros_like(dk_acc)
        dv_acc[...] = jnp.zeros_like(dv_acc)

    for i in range(total // block):
        rows = pl.ds(i * block, block)
        width = (i + 1) * block
        q = q_ref[rows, :]
        o = o_ref[rows, :]
        k = k_ref[pl.ds(0, width), :]
        v = v_ref[pl.ds(0, width), :]
        s = lax.dot_general(k, q, nt, preferred_element_type=jnp.float32)
        key_at = lax.broadcasted_iota(jnp.int32, (width, block), 0)
        query_at = i * block + lax.broadcasted_iota(jnp.int32, (1, block), 1)
        allowed = (key_at <= query_at) & (key_at >= start_ref[:, rows])
        s = jnp.where(allowed, s, -jnp.inf)
        top = jnp.max(s, axis=0, keepdims=True)
        expo = jnp.exp2((s - top) * (scale * math.log2(math.e)))
        prob = expo * (1.0 / jnp.sum(expo, axis=0, keepdims=True))
        dprob = lax.dot_general(v, o, nt, preferred_element_type=jnp.float32)
        delta = jnp.sum(prob * dprob, axis=0, keepdims=True)
        dscore = (prob * ((dprob - delta) * scale)).astype(jnp.bfloat16)
        dq = lax.dot_general(dscore, k, tn, preferred_element_type=jnp.float32)
        out_ref[rows, pl.ds(pl.multiple_of(head * HD, HD), HD)] = dq.astype(jnp.bfloat16)
        dk_acc[pl.ds(0, width), :] += jnp.dot(dscore, q, preferred_element_type=jnp.float32)
        dv_acc[pl.ds(0, width), :] += jnp.dot(
            prob.astype(jnp.bfloat16), o, preferred_element_type=jnp.float32
        )

    @pl.when(head == heads - 1)
    def _():
        out_ref[:, pl.ds(heads * HD, HD)] = dk_acc[...].astype(jnp.bfloat16)
        out_ref[:, pl.ds((heads + 1) * HD, HD)] = dv_acc[...].astype(jnp.bfloat16)


def attend(start, q_all, o_all, k_head, v_head):
    total, width = q_all.shape
    heads = width // HD
    block = min(256, total)
    one_head = pl.BlockSpec((total, HD), lambda h: (0, h))
    shared = pl.BlockSpec((total, HD), lambda h: (0, 0))
    return pl.pallas_call(
        functools.partial(attend_kernel, heads=heads, block=block),
        grid=(heads,),
        in_specs=[pl.BlockSpec((1, total), lambda h: (0, 0)), one_head, one_head, shared, shared],
        out_specs=pl.BlockSpec((total, (heads + 2) * HD), lambda h: (0, 0)),
        out_shape=jax.ShapeDtypeStruct((total, (heads + 2) * HD), jnp.bfloat16),
        scratch_shapes=[pltpu.VMEM((total, HD), jnp.float32), pltpu.VMEM((total, HD), jnp.float32)],
        compiler_params=pltpu.CompilerParams(dimension_semantics=("arbitrary",)),
        name="attend",
    )(start, q_all, o_all, k_head, v_head)


def body(queries, keys, values, out_grad, documents, query_weight, key_weight, value_weight):
    count = lax.axis_size("seq")
    tok = queries.shape[1]
    total = tok * count
    features = query_weight.shape[1]
    kv = keys.shape[2] // HD
    reps = count // kv
    slot_head = lax.axis_index("seq") // reps

    def by_heads(x):
        parts = x.reshape(tok, count, -1).transpose(1, 0, 2)
        got = lax.all_to_all(parts, "seq", split_axis=0, concat_axis=0, tiled=True)
        return got.reshape(total, -1)

    def by_kv_head(x):
        return by_heads(jnp.repeat(x.reshape(tok, kv, HD), reps, axis=1))

    k_head = by_kv_head(keys[0])
    v_head = by_kv_head(values[0])
    q_all = by_heads(queries[0])
    o_all = by_heads(out_grad[0])
    ids = documents[0]
    start = jnp.sum((ids[:, None] < ids[None, :]).astype(jnp.int32), axis=0, keepdims=True)
    grads = attend(start, q_all, o_all, k_head, v_head)

    def rows_of(weight):
        return lax.dynamic_slice_in_dim(weight[0], slot_head * HD, HD, 0)

    weight = jnp.concatenate([query_weight[0], rows_of(key_weight), rows_of(value_weight)], axis=0)
    model = weight.shape[1]
    step = model // CHUNKS
    received = []
    for c in range(CHUNKS):
        part = jnp.dot(
            grads, weight[:, c * step : (c + 1) * step], preferred_element_type=jnp.float32
        ).astype(jnp.bfloat16)
        dinput = lax.psum_scatter(part, "seq", scatter_dimension=0, tiled=True)
        received.append(passed_along(dinput, "section", -1))
    return jnp.concatenate(received, axis=1)[None]


def solution(mesh):
    in_specs = (
        P("section", "seq", None),
        P("section", "seq", None),
        P("section", "seq", None),
        P("section", "seq", None),
        P("section", None),
        P("section", "seq", None),
        P("section", None, None),
        P("section", None, None),
    )
    out_specs = P("section", "seq", None)
    return jax.shard_map(body, mesh=mesh, in_specs=in_specs, out_specs=out_specs, check_vma=False)
```

time: 435 us -> 246 us (0.57)
  matrix products: 133 us -> 14.7 us
  waiting for transfers between devices: 199 us -> 159 us
  local copies, waits for them, and re-layouts: 46.1 us -> 12.3 us
  Pallas kernels: 0 us -> 16.8 us
  starting transfers between devices: 30.2 us -> 19.8 us
    all_to_all x7 -> x4, waiting for transfers between devices: 173 us -> 55.8 us  [by_heads(): got = lax.all_to_all(parts, 'seq', split_axis=0, concat_axis=0, tiled=True)]
    dot_general x11 -> x2, matrix products: 118 us -> 14.7 us  [body(): jnp.dot(grads, weight[:, c * step:(c + 1) * step], preferred_element_type...]
    reduce_scatter x0 -> x2, waiting for transfers between devices: none -> 90.2 us  [body(): dinput = lax.psum_scatter(part, 'seq', scatter_dimension=0, tiled=True)]
    pallas_call x0 -> x1, Pallas kernels: none -> 16.8 us  [attend(): pl.pallas_call(functools.partial(attend_kernel, heads=heads, block=block)...]
    sub x2 -> x0, matrix products: 14.8 us -> none  [attend(): expo = jnp.exp(scores - top)]
    ppermute x1 -> x2, waiting for transfers between devices: 25.3 us -> 12.6 us  [passed_along(): return lax.ppermute(block, axis, route)]
    all_to_all x7 -> x4, starting transfers between devices: 28.9 us -> 17.1 us  [by_heads(): got = lax.all_to_all(parts, 'seq', split_axis=0, concat_axis=0, tiled=True)]
    broadcast_in_dim x4 -> x2, local copies, waits for them, and re-layouts: 12.2 us -> 1.52 us  [by_kv_head(): return by_heads(jnp.repeat(x.reshape(tok, kv, HD), reps, axis=1))]
  transfers between devices with their start and end apart: 9 -> 8, of which waited for: 8 -> 7; matrix products, arithmetic and copies ran while one was open for 40% -> 9% of each run, Pallas kernels for 0% -> 0%
where the time goes in v1:
time: 246 us
  waiting for transfers between devices  159 us (65%)
  starting transfers between devices  19.8 us (8%)
  Pallas kernels  16.8 us (7%)
  matrix products  14.7 us (6%)
  between operations  13.6 us (6%)
  local copies, waits for them, and re-layouts  12.3 us (5%)
  other arithmetic  9.99 us (4%)
    reduce_scatter x2, waiting for transfers between devices, body(): dinput = lax.psum_scatter(part, 'seq', scatter_dimension=0, tiled=True)  90.2 us
    all_to_all x4, waiting for transfers between devices, by_heads(): got = lax.all_to_all(parts, 'seq', split_axis=0, concat_axis=0, tiled=True)  55.8 us
    all_to_all x4, starting transfers between devices, by_heads(): got = lax.all_to_all(parts, 'seq', split_axis=0, concat_axis=0, tiled=True)  17.1 us
    pallas_call x1, Pallas kernels, attend(): pl.pallas_call(functools.partial(attend_kernel, heads=heads, block=block)...  16.8 us
    dot_general x2, matrix products, body(): jnp.dot(grads, weight[:, c * step:(c + 1) * step], preferred_element_type...  14.7 us
    ppermute x2, waiting for transfers between devices, passed_along(): return lax.ppermute(block, axis, route)  12.6 us
    concatenate x1, other arithmetic, body(): jnp.concatenate([query_weight[0], rows_of(key_weight), rows_of(value_weig...  7.86 us
  transfers between devices with their start and end apart: 8, of which 7 were waited for; matrix products, arithmetic and copies ran while one was open for 9% of the time, Pallas kernels for 0%

profile of v1, /device:TPU:0, one launch (start us, length us, event | category | flops | bytes accessed | tf_op | source)
XLA Modules:
  0.0 245.6 jit_solution(4688968086129168096)
XLA Ops:
  6.5 0.9 reshape_squeeze.15
  7.5 0.7 broadcast_in_dim.14
  8.2 0.0 copy-start.6
  8.2 6.5 %all-to-all-start.3 = ((bf16[8,128,128]{2,1,0:T(8,128)(2,1)}), bf16[8,128,128]{2,1,0:T(8,128)(2,1)S(1)}, u32[]{:S(2)}, u32[]{:S(2)}) async-start(bf16[8,128,128]{2,1,0:T(8,128)(2,1)} %bitcast.10), calls=%async_computation.3 | async-start | bytes 524288 | tf_op jit(solution)/shard_map/all_to_all | solution.py:93
  14.7 0.9 reshape_squeeze.14
  15.7 8.7 %all-to-all-done.3 = bf16[8,128,128]{2,1,0:T(8,128)(2,1)S(1)} async-done(((bf16[8,128,128]{2,1,0:T(8,128)(2,1)}), bf16[8,128,128]{2,1,0:T(8,128)(2,1)S(1)}, u32[]{:S(2)}, u32[]{:S(2)}) %all-to-all-start.3) | async-done | bytes 262176 | tf_op jit(solution)/shard_map/all_to_all | solution.py:93
  24.4 0.0 copy-start.4
  24.4 0.8 broadcast_in_dim.13
  25.2 3.4 %all-to-all-start.2 = ((bf16[8,128,128]{2,1,0:T(8,128)(2,1)}), bf16[8,128,128]{2,1,0:T(8,128)(2,1)S(1)}, u32[]{:S(2)}, u32[]{:S(2)}) async-start(bf16[8,128,128]{2,1,0:T(8,128)(2,1)} %bitcast.7), calls=%async_computation.2 | async-start | bytes 524288 | tf_op jit(solution)/shard_map/all_to_all | solution.py:93
  28.6 1.6 copy.17
  30.3 1.3 copy.22
  31.5 6.7 %all-to-all-done.2 = bf16[8,128,128]{2,1,0:T(8,128)(2,1)S(1)} async-done(((bf16[8,128,128]{2,1,0:T(8,128)(2,1)}), bf16[8,128,128]{2,1,0:T(8,128)(2,1)S(1)}, u32[]{:S(2)}, u32[]{:S(2)}) %all-to-all-start.2) | async-done | bytes 262176 | tf_op jit(solution)/shard_map/all_to_all | solution.py:93
  38.3 0.0 copy-start.5
  38.3 0.0 copy-start.7
  38.3 3.7 %all-to-all-start = ((bf16[8,128,512]{2,1,0:T(8,128)(2,1)}), bf16[8,128,512]{2,1,0:T(8,128)(2,1)S(1)}, u32[]{:S(2)}, u32[]{:S(2)}) async-start(bf16[8,128,512]{2,1,0:T(8,128)(2,1)} %bitcast.32), calls=%async_computation | async-start | bytes 2097152 | tf_op jit(solution)/shard_map/all_to_all | solution.py:93
  42.0 0.0 copy-done.6
  42.0 0.4 copy.18
  42.4 0.0 copy-done.4
  42.4 1.3 copy.21
  43.7 24.8 %all-to-all-done = bf16[8,128,512]{2,1,0:T(8,128)(2,1)S(1)} async-done(((bf16[8,128,512]{2,1,0:T(8,128)(2,1)}), bf16[8,128,512]{2,1,0:T(8,128)(2,1)S(1)}, u32[]{:S(2)}, u32[]{:S(2)}) %all-to-all-start) | async-done | bytes 1048608 | tf_op jit(solution)/shard_map/all_to_all | solution.py:93
  68.5 0.0 copy-start.1
  68.5 0.0 copy-done.5
  68.5 3.6 %all-to-all-start.1 = ((bf16[8,128,512]{2,1,0:T(8,128)(2,1)}), bf16[8,128,512]{2,1,0:T(8,128)(2,1)S(1)}, u32[]{:S(2)}, u32[]{:S(2)}) async-start(bf16[8,128,512]{2,1,0:T(8,128)(2,1)} %bitcast.31), calls=%async_computation.1 | async-start | bytes 2097152 | tf_op jit(solution)/shard_map/all_to_all | solution.py:93
  72.0 0.0 reduce-scatter.3.cloned.1.call-start
  72.1 0.0 copy-start
  72.1 0.0 copy-done.7
  72.1 1.1 convert_reduce_fusion
  73.2 1.9 dynamic-slice_bitcast_fusion
  75.1 0.0 copy-done
  75.1 7.9 %pad_maximum_fusion = bf16[768,4096]{1,0:T(8,128)(2,1)} fusion(bf16[128,4096]{1,0:T(8,128)(2,1)S(1)} %get-tuple-element.5, bf16[128,4096]{1,0:T(8,128)(2,1)S(1)} %get-tuple-element.6, bf16[512,4096]{1,0:T(8,128)(2,1)S(1)} %bitcast.33), kind=kLoop, calls=%fused_computation | loop fusion | flops 18874368 | bytes 12582912 | tf_op jit(solution)/shard_map/concatenate | solution.py:110
  83.0 0.0 copy-done.1
  83.0 15.5 %all-to-all-done.1 = bf16[8,128,512]{2,1,0:T(8,128)(2,1)S(1)} async-done(((bf16[8,128,512]{2,1,0:T(8,128)(2,1)}), bf16[8,128,512]{2,1,0:T(8,128)(2,1)S(1)}, u32[]{:S(2)}, u32[]{:S(2)}) %all-to-all-start.1) | async-done | bytes 1048608 | tf_op jit(solution)/shard_map/all_to_all | solution.py:93
  98.5 0.0 copy-start.2
  98.5 1.0 copy-done.2
  99.5 16.8 %attend.1 = bf16[1024,768]{1,0:T(8,128)(2,1)} custom-call(s32[1,1024]{1,0:T(1,128)} %bitcast.42, bf16[1024,512]{1,0:T(8,128)(2,1)} %bitcast.34, bf16[1024,512]{1,0:T(8,128)(2,1)} %bitcast.35, bf16[1024,128]{1,0:T(8,128)(2,1)} %bitcast.39, bf16[1024,128]{1,0:T(8,128)(2,1)} %bitcast.38), custom_call_target="tpu_custom_call" | custom-call | tf_op jit(solution)/shard_map/attend/pallas_call | solution.py:70
  116.3 7.8 %convolution_convert_fusion.1 = bf16[1024,2048]{1,0:T(8,128)(2,1)} fusion(bf16[1024,768]{1,0:T(8,128)(2,1)} %attend.1, bf16[768,4096]{1,0:T(8,128)(2,1)} %pad_maximum_fusion), kind=kOutput, calls=%fused_computation.3 | convolution fusion | flops 3223322624 | bytes 8912896 | tf_op jit(solution)/shard_map/dot_general | solution.py:115
  124.1 0.0 copy-start.3
  124.1 0.0 reduce-scatter.3.cloned.1.call-update
  124.2 0.0 reduce-scatter.5.cloned.1.call-start
  124.2 1.3 copy-done.3
  125.5 6.8 %convolution_convert_fusion = bf16[1024,2048]{1,0:T(8,128)(2,1)} fusion(bf16[1024,768]{1,0:T(8,128)(2,1)S(1)} %copy-done.3, bf16[768,4096]{1,0:T(8,128)(2,1)} %pad_maximum_fusion), kind=kOutput, calls=%fused_computation.2 | convolution fusion | flops 3223322624 | bytes 8912896 | tf_op jit(solution)/shard_map/dot_general | solution.py:115
  132.4 0.0 reduce-scatter.5.cloned.1.call-update
  132.4 40.7 %reduce-scatter.3.cloned.1.call-done = bf16[128,2048]{1,0:T(8,128)(2,1)} async-done(((bf16[1024,2048]{1,0:T(8,128)(2,1)}), bf16[128,2048]{1,0:T(8,128)(2,1)}) %reduce-scatter.3.cloned.1.call-update) | async-done | bytes 524304 | tf_op jit(solution)/shard_map/reduce_scatter | solution.py:118
  173.1 1.3 collective-permute-start
  174.4 49.5 %reduce-scatter.5.cloned.1.call-done = bf16[128,2048]{1,0:T(8,128)(2,1)} async-done(((bf16[1024,2048]{1,0:T(8,128)(2,1)}), bf16[128,2048]{1,0:T(8,128)(2,1)}) %reduce-scatter.5.cloned.1.call-update) | async-done | bytes 524304 | tf_op jit(solution)/shard_map/reduce_scatter | solution.py:118
  223.9 1.3 collective-permute-start.1
  225.2 0.0 collective-permute-done
  225.2 12.6 %collective-permute-done.1 = bf16[128,2048]{1,0:T(8,128)(2,1)S(1)} collective-permute-done((bf16[128,2048]{1,0:T(8,128)(2,1)}, bf16[128,2048]{1,0:T(8,128)(2,1)S(1)}, u32[]{:S(2)}, u32[]{:S(2)}) %collective-permute-start.1) | collective-permute-done | bytes 524320 | tf_op jit(solution)/shard_map/ppermute | solution.py:18
  237.7 1.1 maximum_bitcast_fusion
  (2 shorter events, 0.0 us)
Async XLA Ops:
  8.2 33.7 %copy-start.6 = (bf16[1,128,4096]{2,1,0:T(8,128)(2,1)S(1)}, bf16[1,128,4096]{2,1,0:T(8,128)(2,1)}, u32[]{:S(2)}) copy-start(bf16[1,128,4096]{2,1,0:T(8,128)(2,1)} %param.11) | copy-start | bytes 3145732
  8.2 16.2 %all-to-all-start.3 = ((bf16[8,128,128]{2,1,0:T(8,128)(2,1)}), bf16[8,128,128]{2,1,0:T(8,128)(2,1)S(1)}, u32[]{:S(2)}, u32[]{:S(2)}) async-start(bf16[8,128,128]{2,1,0:T(8,128)(2,1)} %bitcast.10), calls=%async_computation.3 | async-start | bytes 524288 | tf_op jit(solution)/shard_map/all_to_all | solution.py:93
  24.4 18.0 %copy-start.4 = (bf16[8,128,128]{2,1,0:T(8,128)(2,1)}, bf16[8,128,128]{2,1,0:T(8,128)(2,1)S(1)}, u32[]{:S(2)}) copy-start(bf16[8,128,128]{2,1,0:T(8,128)(2,1)S(1)} %all-to-all-done.3) | copy-start | bytes 786436
  25.2 13.1 %all-to-all-start.2 = ((bf16[8,128,128]{2,1,0:T(8,128)(2,1)}), bf16[8,128,128]{2,1,0:T(8,128)(2,1)S(1)}, u32[]{:S(2)}, u32[]{:S(2)}) async-start(bf16[8,128,128]{2,1,0:T(8,128)(2,1)} %bitcast.7), calls=%async_computation.2 | async-start | bytes 524288 | tf_op jit(solution)/shard_map/all_to_all | solution.py:93
  38.3 30.2 %copy-start.5 = (bf16[8,128,128]{2,1,0:T(8,128)(2,1)}, bf16[8,128,128]{2,1,0:T(8,128)(2,1)S(1)}, u32[]{:S(2)}) copy-start(bf16[8,128,128]{2,1,0:T(8,128)(2,1)S(1)} %all-to-all-done.2) | copy-start | bytes 786436
  38.3 33.8 %copy-start.7 = (s32[1,1024]{1,0:T(1,128)S(1)}, s32[1,1024]{1,0:T(1,128)}, u32[]{:S(2)}) copy-start(s32[1,1024]{1,0:T(1,128)} %param.12) | copy-start | bytes 12292
  38.3 30.2 %all-to-all-start = ((bf16[8,128,512]{2,1,0:T(8,128)(2,1)}), bf16[8,128,512]{2,1,0:T(8,128)(2,1)S(1)}, u32[]{:S(2)}, u32[]{:S(2)}) async-start(bf16[8,128,512]{2,1,0:T(8,128)(2,1)} %bitcast.32), calls=%async_computation | async-start | bytes 2097152 | tf_op jit(solution)/shard_map/all_to_all | solution.py:93
  68.5 14.5 %copy-start.1 = (bf16[8,128,512]{2,1,0:T(8,128)(2,1)}, bf16[8,128,512]{2,1,0:T(8,128)(2,1)S(1)}, u32[]{:S(2)}) copy-start(bf16[8,128,512]{2,1,0:T(8,128)(2,1)S(1)} %all-to-all-done) | copy-start | bytes 3145732
  68.5 30.1 %all-to-all-start.1 = ((bf16[8,128,512]{2,1,0:T(8,128)(2,1)}), bf16[8,128,512]{2,1,0:T(8,128)(2,1)S(1)}, u32[]{:S(2)}, u32[]{:S(2)}) async-start(bf16[8,128,512]{2,1,0:T(8,128)(2,1)} %bitcast.31), calls=%async_computation.1 | async-start | bytes 2097152 | tf_op jit(solution)/shard_map/all_to_all | solution.py:93
  72.0 101.1 %reduce-scatter.3.cloned.1.call-start = ((), (), s32[]{:S(2)}) async-start(), calls=%async_computation.6 | async-start | bytes 4718592 | tf_op jit(solution)/shard_map/reduce_scatter | solution.py:118
  72.1 3.0 %copy-start = (bf16[1,512,4096]{2,1,0:T(8,128)(2,1)S(1)}, bf16[1,512,4096]{2,1,0:T(8,128)(2,1)}, u32[]{:S(2)}) copy-start(bf16[1,512,4096]{2,1,0:T(8,128)(2,1)} %param.13) | copy-start | bytes 12582916
  98.5 1.0 copy-start.2
  124.1 1.4 copy-start.3
  124.2 99.7 %reduce-scatter.5.cloned.1.call-start = ((), (), s32[]{:S(2)}) async-start(), calls=%async_computation.7 | async-start | bytes 4718592 | tf_op jit(solution)/shard_map/reduce_scatter | solution.py:118
  173.1 52.0 %collective-permute-start = (bf16[128,2048]{1,0:T(8,128)(2,1)}, bf16[128,2048]{1,0:T(8,128)(2,1)S(1)}, u32[]{:S(2)}, u32[]{:S(2)}) collective-permute-start(bf16[128,2048]{1,0:T(8,128)(2,1)} %reduce-scatter.3.cloned.1.call-done), channel_id=1, source_target_pairs={{8,0},{16,8},{24,16},{9,1},{17,9},{25,17},{10,2},{18,10},{26,18},{... | collective-permute-start | bytes 1572872 | tf_op jit(solution)/shard_map/ppermute | solution.py:18
  223.9 13.9 %collective-permute-start.1 = (bf16[128,2048]{1,0:T(8,128)(2,1)}, bf16[128,2048]{1,0:T(8,128)(2,1)S(1)}, u32[]{:S(2)}, u32[]{:S(2)}) collective-permute-start(bf16[128,2048]{1,0:T(8,128)(2,1)} %reduce-scatter.5.cloned.1.call-done), channel_id=1, source_target_pairs={{8,0},{16,8},{24,16},{9,1},{17,9},{25,17},{10,2},{18,10},{26,18},{... | collective-permute-start | bytes 1572872 | tf_op jit(solution)/shard_map/ppermute | solution.py:18
Sparse Core Ops, SparseCore 0:
  124.3 48.7 reduce-scatter.2
  175.4 48.4 reduce-scatter.4
